TPU v7x, 256 devices: a whole 4x4x8 slice. The times are simulated.
256 devices in a mesh: dp: 16 (over z_hi, x), tp: 16 (over z_lo, y, core).
Axes of the slice: x: 4, y: 4, z: 8 (z_hi: 4, z_lo: 2; z = z_hi * 2 + z_lo), core: 2. Of those that a mesh axis runs over, the one named last changes fastest.
Arguments:
- gradients: bfloat16 [16, 4, 5120, 1280], P('dp', None, 'tp'), may hold values from -6 to 6
- right_factor: float32 [4, 1280, 32], replicated, may hold values from -6 to 6
- weights_before: float32 [4, 5120, 1280], P(None, 'tp', 'dp'), may hold values from -0.15625 to 0.15625
- momentum: float32 [4, 5120, 1280], P(None, 'tp', 'dp'), may hold values from -0.3125 to 0.3125
Outputs:
- new_weights: float32 [4, 5120, 1280], P(None, 'tp', 'dp')
- new_basis: float32 [4, 1280, 32], replicated
- new_momentum: float32 [4, 5120, 1280], P(None, 'tp', 'dp')
All inputs are finite; a program needn't handle non-finite values.
Results may differ from a plain program's by a relative error of at most 0.003.
Values sent between devices are 32-bit elements; how exact they have to be, the bound alone decides.
A program may use at most 64 MiB of HBM per device.

v0:
```python
import jax
import jax.numpy as jnp
from jax import lax
from jax.sharding import PartitionSpec as P

RANK = 32


def split_up(array, dim, devices):
    before, after = (array.shape[:dim], array.shape[dim + 1 :])
    return jnp.moveaxis(array.reshape(*before, devices, -1, *after), dim, 0)


def sum_at_owner(array, axis, dim):
    devices = lax.axis_size(axis)
    pieces = lax.all_to_all(split_up(array, dim, devices), axis, 0, 0, tiled=True)
    return jnp.sum(pieces, axis=0)


def joined_along(pieces, dim):
    lengths = list(pieces.shape[1:])
    lengths[dim] *= pieces.shape[0]
    return jnp.moveaxis(pieces, 0, dim).reshape(lengths)


def from_everyone(array, axis):
    devices = lax.axis_size(axis)
    return lax.all_to_all(
        jnp.broadcast_to(array[None], (devices, *array.shape)), axis, 0, 0, tiled=True
    )


def gather_directly(array, axis, dim):
    return joined_along(from_everyone(array, axis), dim)


def over_copies(array, axis):
    everything = from_everyone(array, axis)
    return jnp.sum(everything, axis=0)


def on_device(gradients, right_factor, weights_before, momentum):
    own_grads = gradients[0]
    part_left = jnp.einsum(
        "liw,lwr->lir",
        own_grads,
        right_factor.astype(jnp.bfloat16),
        preferred_element_type=jnp.float32,
    )
    shares = sum_at_owner(part_left, "dp", 1)
    left = gather_directly(shares, "dp", 1)
    part_gram = jnp.einsum("lir,lis->lrs", left, left, precision=lax.Precision.HIGHEST)
    small_left = left.astype(jnp.bfloat16)
    gram = over_copies(part_gram, "tp")
    part_right = jnp.einsum(
        "liw,lir->lwr", own_grads, small_left, preferred_element_type=jnp.float32
    )
    right = lax.psum(part_right, ("dp", "tp"))
    gram = gram + 0.001 * jnp.mean(jnp.diagonal(gram, axis1=1, axis2=2), axis=1)[
        :, None, None
    ] * jnp.eye(RANK, dtype=jnp.float32)
    place = lax.axis_index("dp") * weights_before.shape[2]
    own_right = lax.dynamic_slice_in_dim(right, place, weights_before.shape[2], axis=1)
    root = jnp.linalg.cholesky(gram)
    half = lax.linalg.triangular_solve(
        root, jnp.swapaxes(own_right, 1, 2), left_side=True, lower=True
    )
    mixed = lax.linalg.triangular_solve(root, half, left_side=True, lower=True, transpose_a=True)
    change = jnp.einsum(
        "lir,lrw->liw", left, mixed, precision=lax.Precision.HIGHEST
    ) / lax.axis_size("dp")
    new_momentum = 0.8 * momentum + change
    new_weights = weights_before - 0.05 * new_momentum
    new_basis = right * lax.rsqrt(jnp.mean(right * right, axis=(1, 2), keepdims=True) + 1e-12)
    return (new_weights, new_basis, new_momentum)


def solution(mesh):
    return jax.shard_map(
        on_device,
        mesh=mesh,
        in_specs=(P("dp", None, "tp", None), P(), P(None, "tp", "dp"), P(None, "tp", "dp")),
        out_specs=(P(None, "tp", "dp"), P(), P(None, "tp", "dp")),
        check_vma=False,
    )
```

profile of v0, /device:TPU:1, one launch (start us, length us, event | category | flops | bytes accessed | tf_op | source)
XLA Modules:
  0.0 371.0 jit_solution(15368953524592591976)
XLA Ops:
  7.2 1.9 copy-done
  9.1 2.0 fusion.2
  11.1 1.7 reshape.46
  12.8 2.6 copy.16
  15.4 2.2 reshape.54
  17.6 11.6 %all-to-all-start = ((f32[16,1,2560]{2,1,0:T(1,128)}), f32[16,1,2560]{2,1,0:T(1,128)S(1)}, u32[]{:S(2)}, u32[]{:S(2)}) async-start(f32[16,1,2560]{2,1,0:T(1,128)} %reshape.54), calls=%async_computation | async-start | bytes 327680 | tf_op jit(solution)/shard_map/all_to_all | solution.py:16
  29.1 9.4 %all-to-all-done = f32[16,1,2560]{2,1,0:T(1,128)S(1)} async-done(((f32[16,1,2560]{2,1,0:T(1,128)}), f32[16,1,2560]{2,1,0:T(1,128)S(1)}, u32[]{:S(2)}, u32[]{:S(2)}) %all-to-all-start) | async-done | bytes 163872 | tf_op jit(solution)/shard_map/all_to_all | solution.py:16
  39.1 1.7 reduce.7
  40.9 2.1 reshape.55
  45.1 2.2 reshape.56
  47.2 4.0 %all-to-all-start.1 = ((f32[16,1,2560]{2,1,0:T(1,128)}), f32[16,1,2560]{2,1,0:T(1,128)S(1)}, u32[]{:S(2)}, u32[]{:S(2)}) async-start(f32[16,1,2560]{2,1,0:T(1,128)} %reshape.56), calls=%async_computation.1 | async-start | bytes 327680 | tf_op jit(solution)/shard_map/all_to_all | solution.py:28
  51.9 8.9 %all-to-all-done.1 = f32[16,1,2560]{2,1,0:T(1,128)S(1)} async-done(((f32[16,1,2560]{2,1,0:T(1,128)}), f32[16,1,2560]{2,1,0:T(1,128)S(1)}, u32[]{:S(2)}, u32[]{:S(2)}) %all-to-all-start.1) | async-done | bytes 163872 | tf_op jit(solution)/shard_map/all_to_all | solution.py:28
  60.9 1.7 reduce.8
  62.6 2.1 reshape.57
  69.0 2.4 reshape.58
  71.4 8.0 %all-to-all-start.2 = ((f32[16,1,4096]{2,1,0:T(1,128)}), f32[16,1,4096]{2,1,0:T(1,128)}, u32[]{:S(2)}, u32[]{:S(2)}) async-start(f32[16,1,4096]{2,1,0:T(1,128)} %reshape.58), calls=%async_computation.2 | async-start | bytes 524288 | tf_op jit(solution)/shard_map/all_to_all | solution.py:28
  79.4 240.9 %all-reduce.2.cloned.1.call-done = f32[4,1280,32]{1,2,0:T(8,128)} async-done(((f32[4,1280,32]{1,2,0:T(8,128)}), f32[4,1280,32]{1,2,0:T(8,128)}) %all-reduce.2.cloned.1.call-update) | async-done | bytes 655376 | tf_op jit(solution)/shard_map/psum | solution.py:58
  321.5 2.0 broadcast_multiply_fusion
  323.5 3.0 reduce.9
  326.5 2.3 reshape.59
  331.8 1.9 gather_fusion
  336.1 12.4 %custom-call.9 = f32[4,32,32]{2,1,0:T(8,128)S(1)} custom-call(f32[4,32,32]{2,1,0:T(8,128)} %fusion.15), custom_call_target="Cholesky" | custom-call | tf_op jit(solution)/shard_map/jit(cholesky)/cholesky | solution.py:64
  349.4 10.5 %custom-call.10 = f32[4,1,32,32]{2,3,1,0:T(8,128)S(1)} custom-call(f32[4,1,32,32]{3,2,1,0:T(8,128)} %select_bitcast_fusion), custom_call_target="InvertDiagBlocksLowerTriangular" | custom-call | tf_op jit(solution)/shard_map/triangular_solve | solution.py:68
  361.4 2.8 multiply_subtract_fusion
  (28 shorter events, 16.7 us)
Async XLA Ops:
  7.2 1.9 copy-start
  17.6 21.0 %all-to-all-start = ((f32[16,1,2560]{2,1,0:T(1,128)}), f32[16,1,2560]{2,1,0:T(1,128)S(1)}, u32[]{:S(2)}, u32[]{:S(2)}) async-start(f32[16,1,2560]{2,1,0:T(1,128)} %reshape.54), calls=%async_computation | async-start | bytes 327680 | tf_op jit(solution)/shard_map/all_to_all | solution.py:16
  47.2 13.6 %all-to-all-start.1 = ((f32[16,1,2560]{2,1,0:T(1,128)}), f32[16,1,2560]{2,1,0:T(1,128)S(1)}, u32[]{:S(2)}, u32[]{:S(2)}) async-start(f32[16,1,2560]{2,1,0:T(1,128)} %reshape.56), calls=%async_computation.1 | async-start | bytes 327680 | tf_op jit(solution)/shard_map/all_to_all | solution.py:28
  51.3 269.0 %all-reduce.2.cloned.1.call-start = ((), (), s32[]{:S(2)}) async-start(), calls=%async_computation.3 | async-start | bytes 1310720 | tf_op jit(solution)/shard_map/psum | solution.py:58
  71.4 252.1 %all-to-all-start.2 = ((f32[16,1,4096]{2,1,0:T(1,128)}), f32[16,1,4096]{2,1,0:T(1,128)}, u32[]{:S(2)}, u32[]{:S(2)}) async-start(f32[16,1,4096]{2,1,0:T(1,128)} %reshape.58), calls=%async_computation.2 | async-start | bytes 524288 | tf_op jit(solution)/shard_map/all_to_all | solution.py:28
Sparse Core Ops, SparseCore 0:
  67.7 252.5 all-reduce.1
where the time goes:
time: 372 us; the launch traced here: 371 us
  waiting for transfers between devices  259 us (70%)
  other arithmetic  39 us (10%)
  local copies, waits for them, and re-layouts  27 us (7%)
  starting transfers between devices  23.6 us (6%)
  between operations  14.1 us (4%)
  matrix products  8.1 us (2%)
    psum x1, waiting for transfers between devices, on_device(): right = lax.psum(part_right, ('dp', 'tp'))  241 us
    unnamed x9, local copies, waits for them, and re-layouts  16 us
    another operation x4, other arithmetic, on_device(): root = jnp.linalg.cholesky(gram)  12.6 us
    all_to_all x2, starting transfers between devices, from_everyone(): lax.all_to_all(jnp.broadcast_to(array[None], (devices, *array.shape)), ax...  12 us
    all_to_all x1, starting transfers between devices, sum_at_owner(): lax.all_to_all(split_up(array, dim, devices), axis, 0, 0, tiled=True)  11.6 us
    another operation x3, other arithmetic, on_device(): lax.linalg.triangular_solve(root, half, left_side=True, lower=True, trans...  11.3 us
    all_to_all x1, waiting for transfers between devices, sum_at_owner(): lax.all_to_all(split_up(array, dim, devices), axis, 0, 0, tiled=True)  9.41 us
    all_to_all x2, waiting for transfers between devices, from_everyone(): lax.all_to_all(jnp.broadcast_to(array[None], (devices, *array.shape)), ax...  8.93 us
  transfers between devices with their start and end apart: 4, of which 3 were waited for; matrix products, arithmetic and copies ran while one was open for 2% of the time, Pallas kernels for 0%

commit v1 on v0

v1 whole, which is shorter than its diff:
```python
import functools

import jax
import jax.numpy as jnp
from jax import lax
from jax.experimental import pallas as pl
from jax.experimental.pallas import tpu as pltpu
from jax.sharding import PartitionSpec as P

MESH = pl.DeviceIdType.MESH
F32 = jnp.float32
BF16 = jnp.bfloat16
HIGH = lax.Precision.HIGHEST

LAYERS = 4
RANK = 32
ROWS = 320
WIDTH = 1280
LANES = LAYERS * RANK
OWN = 80
ROW_PARTS = 1
PARTS = ((0, 2), (2, 3))


def nt_dot(a, b, precision=None):
    return lax.dot_general(
        a, b, (((1,), (1,)), ((), ())), precision=precision, preferred_element_type=F32
    )


def nn_dot(a, b, precision=None):
    return lax.dot_general(
        a, b, (((1,), (0,)), ((), ())), precision=precision, preferred_element_type=F32
    )


def tn_dot(a, b, precision=None):
    return lax.dot_general(
        a, b, (((0,), (0,)), ((), ())), precision=precision, preferred_element_type=F32
    )


def total_of(ref, count):
    value = ref[0]
    for i in range(1, count):
        value = value + ref[i]
    return value


def inverse_blocks(gram):
    row = lax.broadcasted_iota(jnp.int32, (RANK, LANES), 0)
    lane = lax.broadcasted_iota(jnp.int32, (RANK, LANES), 1)
    inner = lane % RANK
    group_r = lax.broadcasted_iota(jnp.int32, (LANES, LANES), 0) // RANK
    group_c = lax.broadcasted_iota(jnp.int32, (LANES, LANES), 1) // RANK
    same = (group_r == group_c).astype(F32)
    diagonal = jnp.where(row == inner, gram, 0.0)
    trace = jnp.sum(diagonal, axis=0, keepdims=True)
    mean = nn_dot(jnp.broadcast_to(trace, (8, LANES)), same, HIGH)[0:1] * (1.0 / RANK)
    a = gram + jnp.where(row == inner, 0.001 * mean, 0.0)
    for k in range(RANK):
        column = jnp.zeros_like(a)
        for l in range(LAYERS):
            at = l * RANK + k
            column = jnp.where(
                lane // RANK == l, jnp.broadcast_to(a[:, at : at + 1], a.shape), column
            )
        pivot = 1.0 / column[k : k + 1, :]
        here = inner == k
        new_row = jnp.where(here[0:1], 1.0, a[k : k + 1, :]) * pivot
        a = jnp.where(row == k, new_row, jnp.where(here, 0.0, a) - column * new_row)
    return a


def exchange(
    g_hbm, rt_hbm, right_out, pt_out,
    g_buf, r_buf, part_left, l1, l2, left_all, gr_src, gr_d2d, gr_yz, gr_full,
    pr, d2d, rs_src, rs, zr, ag, left_t,
    load_sem, l_send, l1_recv, l2_recv, l3_recv, gr_send, gr_recv,
    r_send, r1_recv, r2_recv, r3_recv, r4_recv, r5_recv, out_sem,
):
    d = lax.axis_index("dp")
    t = lax.axis_index("tp")
    x, zh = lax.rem(d, 4), lax.div(d, 4)
    zl, y, c = lax.div(t, 8), lax.rem(lax.div(t, 2), 4), lax.rem(t, 2)
    z = zh * 2 + zl
    chip = x * 4 + y
    yz = zl * 4 + y

    def device(x_, y_, z_, c_):
        return (lax.div(z_, 2) * 4 + x_, lax.rem(z_, 2) * 8 + y_ * 2 + c_)

    def shifted(value, step, size):
        return lax.rem(value + step, size)

    x_peers = [(shifted(x, k, 4), device(shifted(x, k, 4), y, z, c)) for k in (1, 3, 2)]
    zh_peers = [device(x, y, shifted(z, 2 * k, 8), c) for k in (1, 3, 2)]
    z_peers = [device(x, y, shifted(z, k, 8), c) for k in (4, 3, 5, 2, 6, 1, 7)]
    plane_peers = []
    for dx, dy in sorted(
        [(i, j) for i in range(4) for j in range(4) if i or j],
        key=lambda p: -(min(p[0], 4 - p[0]) + min(p[1], 4 - p[1])),
    ):
        x_, y_ = shifted(x, dx, 4), shifted(y, dy, 4)
        plane_peers.append((x_ * 4 + y_, device(x_, y_, z, c)))
    other_z = zh * 2 + (1 - zl)
    yz_peers = [device(x, shifted(y, k, 4), z, c) for k in (1, 2, 3)] + [
        device(x, shifted(y, k, 4), other_z, c) for k in (0, 1, 2, 3)
    ]
    partner = device(x, y, z, 1 - c)

    def send(src, dst, send_sem, recv_sem, to):
        pltpu.make_async_remote_copy(
            src_ref=src, dst_ref=dst, send_sem=send_sem, recv_sem=recv_sem,
            device_id=to, device_id_type=MESH,
        ).start()

    def take(ref, sem):
        pltpu.make_async_copy(ref, ref, sem).wait()

    loads = []
    for l in range(LAYERS):
        a = pltpu.make_async_copy(rt_hbm.at[l], r_buf.at[l], load_sem.at[l])
        b = pltpu.make_async_copy(g_hbm.at[l], g_buf.at[l], load_sem.at[LAYERS + l])
        a.start()
        b.start()
        loads.append((a, b))

    barrier = pltpu.get_barrier_semaphore()
    everyone = [p for _, p in plane_peers] + z_peers + yz_peers[4:] + [partner]
    for p in everyone:
        pl.semaphore_signal(barrier, inc=1, device_id=p, device_id_type=MESH)

    acc = None
    for l in range(LAYERS):
        for copy in loads[l]:
            copy.wait()
        pieces = []
        if l > 0:
            pieces.append(jnp.zeros((l * RANK, WIDTH), BF16))
        pieces.append(r_buf[l].astype(BF16))
        if l < LAYERS - 1:
            pieces.append(jnp.zeros(((LAYERS - 1 - l) * RANK, WIDTH), BF16))
        term = nt_dot(g_buf[l], jnp.concatenate(pieces, axis=0))
        acc = term if acc is None else acc + term
    part_left[...] = acc.reshape(4, ROWS // 4, LANES)

    pl.semaphore_wait(barrier, len(everyone))

    size = ROWS // 4 // ROW_PARTS
    for s in range(ROW_PARTS):
        rows = pl.ds(s * size, size)
        for n, (x_, p) in enumerate(x_peers):
            send(part_left.at[x_, rows], l1.at[x, rows], l_send.at[0], l1_recv.at[s], p)
    l1[x] = part_left[x]
    for s in range(ROW_PARTS):
        rows = pl.ds(s * size, size)
        take(l1.at[pl.ds(0, 3), rows], l1_recv.at[s])
        l2[zh, rows] = l1[0, rows] + l1[1, rows] + l1[2, rows] + l1[3, rows]
        for p in zh_peers:
            send(l2.at[zh, rows], l2.at[zh, rows], l_send.at[1], l2_recv.at[s], p)
    for s in range(ROW_PARTS):
        rows = pl.ds(s * size, size)
        take(l2.at[pl.ds(0, 3), rows], l2_recv.at[s])
        left_all[x, rows] = l2[0, rows] + l2[1, rows] + l2[2, rows] + l2[3, rows]
        for _, p in x_peers:
            send(left_all.at[x, rows], left_all.at[x, rows], l_send.at[2], l3_recv.at[s], p)
    for s in range(ROW_PARTS):
        rows = pl.ds(s * size, size)
        take(left_all.at[pl.ds(0, 3), rows], l3_recv.at[s])

    left = left_all[...].reshape(ROWS, LANES)
    turned = left.T
    left_t[...] = turned
    small = turned.astype(BF16)

    for n, (p0, m) in enumerate(PARTS):
        columns = slice(p0 * 256, (p0 + m) * 256)
        for l in range(LAYERS):
            term = nn_dot(small[l * RANK : (l + 1) * RANK], g_buf[l, :, columns])
            for i in range(2 * m):
                pr[p0 + i // 2, i % 2, l * RANK : (l + 1) * RANK] = term[
                    :, i * 128 : (i + 1) * 128
                ]
        span = pl.ds(p0, m)
        send(pr.at[span, 1 - c], d2d.at[span], r_send.at[0], r1_recv.at[n], partner)

    block = tn_dot(left, left, HIGH)
    lane = lax.broadcasted_iota(jnp.int32, (RANK, LANES), 1) // RANK
    compact = jnp.zeros((RANK, LANES), F32)
    for l in range(LAYERS):
        compact = jnp.where(lane == l, block[l * RANK : (l + 1) * RANK], compact)
    gr_src[...] = compact.reshape(2, RANK // 2, LANES)
    send(gr_src.at[1 - c], gr_d2d, gr_send.at[0], gr_recv.at[0], partner)

    for n, (p0, m) in enumerate(PARTS):
        span = pl.ds(p0, m)
        take(d2d.at[span], r1_recv.at[n])
        rs_src[span] = pr[span, c] + d2d[span]
        for i, p in plane_peers:
            send(
                rs_src.at[span, pl.ds(i * 8, 8)], rs.at[chip, span],
                r_send.at[1], r2_recv.at[n], p,
            )
        rs[chip, span] = rs_src[span, pl.ds(pl.multiple_of(chip * 8, 8), 8)]

    take(gr_d2d, gr_recv.at[0])
    gr_yz[yz] = gr_src[c] + gr_d2d[...]
    for p in yz_peers:
        send(gr_yz.at[yz], gr_yz.at[yz], gr_send.at[1], gr_recv.at[1], p)

    for n, (p0, m) in enumerate(PARTS):
        span = pl.ds(p0, m)
        take(rs.at[pl.ds(0, 15), span], r2_recv.at[n])
        value = rs[0, span]
        for i in range(1, 16):
            value = value + rs[i, span]
        zr[z, span] = value
        for p in z_peers:
            send(zr.at[z, span], zr.at[z, span], r_send.at[2], r3_recv.at[n], p)

    take(gr_yz.at[pl.ds(0, 7)], gr_recv.at[1])
    gr_full[c] = total_of(gr_yz, 8)
    send(gr_full.at[c], gr_full.at[c], gr_send.at[2], gr_recv.at[2], partner)

    mine = pl.ds(pl.multiple_of(chip * 8, 8), 8)
    for n, (p0, m) in enumerate(PARTS):
        span = pl.ds(p0, m)
        take(zr.at[pl.ds(0, 7), span], r3_recv.at[n])
        value = zr[0, span]
        for i in range(1, 8):
            value = value + zr[i, span]
        ag[span, c, mine] = value
        for _, p in plane_peers:
            send(
                ag.at[span, c, mine], ag.at[span, c, mine], r_send.at[3], r4_recv.at[n], p
            )

    take(gr_full.at[0], gr_recv.at[2])
    inverse = inverse_blocks(gr_full[...].reshape(RANK, LANES))
    spread = jnp.concatenate(
        [jnp.where(lane == l, inverse, 0.0) for l in range(LAYERS)], axis=0
    )
    pt_out[...] = nn_dot(spread, left_t[...], HIGH) * (1.0 / 16)

    outs = []
    for n, (p0, m) in enumerate(PARTS):
        span = pl.ds(p0, m)
        take(ag.at[span, 0, pl.ds(0, 120)], r4_recv.at[n])
        send(ag.at[span, c], ag.at[span, c], r_send.at[4], r5_recv.at[n], partner)
    for n, (p0, m) in enumerate(PARTS):
        span = pl.ds(p0, m)
        take(ag.at[span, 0], r5_recv.at[n])
        for p in range(p0, p0 + m):
            for h in range(2):
                right_out[:, (2 * p + h) * 128 : (2 * p + h + 1) * 128] = ag[p, h]

    for n in range(3):
        take(left_all.at[pl.ds(0, 3)], l_send.at[n])
    take(gr_src.at[0], gr_send.at[0])
    take(gr_yz.at[pl.ds(0, 7)], gr_send.at[1])
    take(gr_full.at[0], gr_send.at[2])
    take(pr.at[:, 0], r_send.at[0])
    take(rs.at[pl.ds(0, 15)], r_send.at[1])
    take(zr.at[pl.ds(0, 7)], r_send.at[2])
    take(rs.at[pl.ds(0, 15)], r_send.at[3])
    take(pr.at[:, 0], r_send.at[4])


def finish(right_ref, pt_ref, w_ref, m_ref, new_w_ref, new_b_ref, new_m_ref):
    d = lax.axis_index("dp")
    place = d * OWN
    first = jnp.minimum(lax.div(place, 128), WIDTH // 128 - 2)
    window = right_ref[:, pl.ds(pl.multiple_of(first * 128, 128), 256)]
    offset = place - first * 128
    own = pltpu.roll(window, lax.rem(256 - offset, 256), 1)[:, :128]
    turned = own.T[:OWN]
    lane = lax.broadcasted_iota(jnp.int32, (OWN, LANES), 1) // RANK
    stacked = jnp.concatenate(
        [jnp.where(lane == l, turned, 0.0) for l in range(LAYERS)], axis=0
    )
    change = nn_dot(stacked, pt_ref[...], HIGH)
    for l in range(LAYERS):
        new_m = 0.8 * m_ref[l] + change[l * OWN : (l + 1) * OWN]
        new_m_ref[l] = new_m
        new_w_ref[l] = w_ref[l] - 0.05 * new_m
        part = right_ref[l * RANK : (l + 1) * RANK]
        mean = jnp.sum(part * part) * (1.0 / (RANK * WIDTH))
        new_b_ref[l] = part * lax.rsqrt(jnp.full((1, 1), mean + 1e-12, F32))


def on_device(gradients, right_factor, weights_before, momentum):
    anywhere = pl.BlockSpec(memory_space=pl.ANY)
    vmem = pl.BlockSpec(memory_space=pltpu.VMEM)
    dma = pltpu.SemaphoreType.DMA
    parts = len(PARTS)
    right, pt = pl.pallas_call(
        exchange,
        out_shape=(
            jax.ShapeDtypeStruct((LANES, WIDTH), F32),
            jax.ShapeDtypeStruct((LANES, ROWS), F32),
        ),
        in_specs=[anywhere, anywhere],
        out_specs=[vmem, vmem],
        scratch_shapes=[
            pltpu.VMEM((LAYERS, ROWS, WIDTH), BF16),
            pltpu.VMEM((LAYERS, RANK, WIDTH), F32),
            pltpu.VMEM((4, ROWS // 4, LANES), F32),
            pltpu.VMEM((4, ROWS // 4, LANES), F32),
            pltpu.VMEM((4, ROWS // 4, LANES), F32),
            pltpu.VMEM((4, ROWS // 4, LANES), F32),
            pltpu.VMEM((2, RANK // 2, LANES), F32),
            pltpu.VMEM((RANK // 2, LANES), F32),
            pltpu.VMEM((8, RANK // 2, LANES), F32),
            pltpu.VMEM((2, RANK // 2, LANES), F32),
            pltpu.VMEM((5, 2, LANES, 128), F32),
            pltpu.VMEM((5, LANES, 128), F32),
            pltpu.VMEM((5, LANES, 128), F32),
            pltpu.VMEM((16, 5, 8, 128), F32),
            pltpu.VMEM((8, 5, 8, 128), F32),
            pltpu.VMEM((5, 2, LANES, 128), F32),
            pltpu.VMEM((LANES, ROWS), F32),
            dma((2 * LAYERS,)),
            dma((3,)),
            dma((ROW_PARTS,)),
            dma((ROW_PARTS,)),
            dma((ROW_PARTS,)),
            dma((3,)),
            dma((3,)),
            dma((5,)),
            dma((parts,)),
            dma((parts,)),
            dma((parts,)),
            dma((parts,)),
            dma((parts,)),
            dma((1,)),
        ],
        compiler_params=pltpu.CompilerParams(
            collective_id=0, has_side_effects=True, vmem_limit_bytes=32 << 20
        ),
        name="exchange",
    )(gradients[0], jnp.swapaxes(right_factor, 1, 2))
    new_w, new_b, new_m = pl.pallas_call(
        finish,
        out_shape=(
            jax.ShapeDtypeStruct((LAYERS, OWN, ROWS), F32),
            jax.ShapeDtypeStruct((LAYERS, RANK, WIDTH), F32),
            jax.ShapeDtypeStruct((LAYERS, OWN, ROWS), F32),
        ),
        in_specs=[vmem] * 4,
        out_specs=[vmem] * 3,
        name="finish",
        compiler_params=pltpu.CompilerParams(vmem_limit_bytes=24 << 20),
    )(right, pt, jnp.swapaxes(weights_before, 1, 2), jnp.swapaxes(momentum, 1, 2))
    return (
        jnp.swapaxes(new_w, 1, 2),
        jnp.swapaxes(new_b, 1, 2),
        jnp.swapaxes(new_m, 1, 2),
    )


def solution(mesh):
    return jax.shard_map(
        on_device,
        mesh=mesh,
        in_specs=(P("dp", None, "tp", None), P(), P(None, "tp", "dp"), P(None, "tp", "dp")),
        out_specs=(P(None, "tp", "dp"), P(), P(None, "tp", "dp")),
        check_vma=False,
    )
```

time: 372 us -> 52.2 us (0.14)
  waiting for transfers between devices: 259 us -> 0 us
  Pallas kernels: 0 us -> 48.4 us
  other arithmetic: 39 us -> 0 us
  local copies, waits for them, and re-layouts: 27 us -> 3.01 us
  starting transfers between devices: 23.6 us -> 0 us
  between operations: 14.1 us -> 0.67 us
  matrix products: 8.1 us -> 0 us
    psum x1 -> x0, waiting for transfers between devices: 241 us -> none  [on_device(): right = lax.psum(part_right, ('dp', 'tp'))]
    pallas_call x0 -> x2, Pallas kernels: none -> 48.4 us  [the longest x1 46.5 us: on_device(): pl.pallas_call(exchange, out_shape=(jax.ShapeDtypeStruct((LANES, WIDTH),...]
    another operation x7 -> x0, other arithmetic: 23.8 us -> none  [the longest x4 12.6 us: on_device(): root = jnp.linalg.cholesky(gram)]
    all_to_all x3 -> x0, starting transfers between devices: 23.5 us -> none  [the longest x2 12 us: from_everyone(): lax.all_to_all(jnp.broadcast_to(array[None], (devices, *array.shape)), ax...]
    all_to_all x3 -> x0, waiting for transfers between devices: 18.3 us -> none  [the longest x1 9.41 us: sum_at_owner(): lax.all_to_all(split_up(array, dim, devices), axis, 0, 0, tiled=True)]
    unnamed x9 -> x8, local copies, waits for them, and re-layouts: 16 us -> 3.01 us
    dot_general x4 -> x0, matrix products: 6.66 us -> none  [the longest x1 2.78 us: on_device(): jnp.einsum('lir,lrw->liw', left, mixed, precision=lax.Precision.HIGHEST)]
    all_to_all x3 -> x0, other arithmetic: 6.42 us -> none  [the longest x2 4.69 us: from_everyone(): lax.all_to_all(jnp.broadcast_to(array[None], (devices, *array.shape)), ax...]
  transfers between devices with their start and end apart: 4 -> 0, of which waited for: 3 -> 0; matrix products, arithmetic and copies ran while one was open for 2% -> 0% of each run, Pallas kernels for 0% -> 0%
where the time goes in v1:
time: 52.2 us; the launch traced here: 52.1 us
  Pallas kernels  48.4 us (93%)
  local copies, waits for them, and re-layouts  3.01 us (6%)
  between operations  0.67 us (1%)
    pallas_call x1, Pallas kernels, on_device(): pl.pallas_call(exchange, out_shape=(jax.ShapeDtypeStruct((LANES, WIDTH),...  46.5 us
    unnamed x8, local copies, waits for them, and re-layouts  3.01 us
    pallas_call x1, Pallas kernels, on_device(): pl.pallas_call(finish, out_shape=(jax.ShapeDtypeStruct((LAYERS, OWN, ROWS...  1.9 us

profile of v1, /device:TPU:1, one launch (start us, length us, event | category | flops | bytes accessed | tf_op | source)
XLA Modules:
  0.0 52.1 jit_solution(16135990169875356458)
XLA Ops:
  0.6 0.0 copy-start
  0.6 1.9 %copy-done = bf16[1,4,320,1280]{3,2,1,0:T(8,128)(2,1)S(1)} copy-done((bf16[1,4,320,1280]{3,2,1,0:T(8,128)(2,1)S(1)}, bf16[1,4,320,1280]{3,2,1,0:T(8,128)(2,1)}, u32[]{:S(2)}) %copy-start) | copy-done | bytes 3276824
  2.6 0.0 copy-start.1
  2.6 1.1 %copy-done.1 = f32[4,1280,32]{1,2,0:T(8,128)S(1)} copy-done((f32[4,1280,32]{1,2,0:T(8,128)S(1)}, f32[4,1280,32]{1,2,0:T(8,128)}, u32[]{:S(2)}) %copy-start.1) | copy-done | bytes 655384
  3.6 0.0 copy-start.2
  3.6 0.0 copy-start.3
  3.7 46.5 %exchange.1 = (f32[128,1280]{1,0:T(8,128)S(1)}, f32[128,320]{1,0:T(8,128)S(1)}) custom-call(bf16[4,320,1280]{2,1,0:T(8,128)(2,1)S(1)} %bitcast.7, f32[4,32,1280]{2,1,0:T(8,128)S(1)} %bitcast.8), custom_call_target="tpu_custom_call" | custom-call | tf_op jit(solution)/shard_map/exchange/pallas_call | solution.py:297
  50.2 0.0 copy-done.2
  50.2 0.0 copy-done.3
  50.2 1.9 %finish.1 = (f32[4,80,320]{2,1,0:T(8,128)}, f32[4,32,1280]{2,1,0:T(8,128)}, f32[4,80,320]{2,1,0:T(8,128)}) custom-call(f32[128,1280]{1,0:T(8,128)S(1)} %get-tuple-element.8.right_ref, f32[128,320]{1,0:T(8,128)S(1)} %get-tuple-element.9.pt_ref, f32[4,80,320]{2,1,0:T(8,128)S(1)} %bitcast.9, f32[4,80,320]{2,1,0:T(8,128)S(1)} %bitcast.10), custom_call_target="tpu_custom_call" | custom-call | tf_op jit(solution)/shard_map/finish/pallas_call | solution.py:343
Async XLA Ops:
  0.6 1.9 %copy-start = (bf16[1,4,320,1280]{3,2,1,0:T(8,128)(2,1)S(1)}, bf16[1,4,320,1280]{3,2,1,0:T(8,128)(2,1)}, u32[]{:S(2)}) copy-start(bf16[1,4,320,1280]{3,2,1,0:T(8,128)(2,1)} %param.4) | copy-start | bytes 9830404
  2.6 1.1 %copy-start.1 = (f32[4,1280,32]{1,2,0:T(8,128)S(1)}, f32[4,1280,32]{1,2,0:T(8,128)}, u32[]{:S(2)}) copy-start(f32[4,1280,32]{1,2,0:T(8,128)} %param.5) | copy-start | bytes 1966084
  3.6 46.5 %copy-start.2 = (f32[4,320,80]{1,2,0:T(8,128)S(1)}, f32[4,320,80]{1,2,0:T(8,128)}, u32[]{:S(2)}) copy-start(f32[4,320,80]{1,2,0:T(8,128)} %param.6) | copy-start | bytes 1228804
  3.6 46.5 %copy-start.3 = (f32[4,320,80]{1,2,0:T(8,128)S(1)}, f32[4,320,80]{1,2,0:T(8,128)}, u32[]{:S(2)}) copy-start(f32[4,320,80]{1,2,0:T(8,128)} %param.7) | copy-start | bytes 1228804
